TPU v7x, 32 devices: a whole 2x2x4 slice. The times are simulated.
32 devices in a mesh: zero: 16 (over z, y, core), width: 2 (over x).
Axes of the slice: x: 2, y: 2, z: 4, core: 2. Of those that a mesh axis runs over, the one named last changes fastest.
Arguments:
- slopes_in: float32 [128, 128, 4096], P(None, 'zero', 'width'), may hold values from -6 to 6
- moments_in: float32 [128, 128, 4096], P(None, 'zero', 'width'), may hold values from -6 to 6
- weights_in: float32 [128, 128, 4096], P(None, 'zero', 'width'), may hold values from -0.1875 to 0.1875
Outputs:
- new_weights: float32 [128, 128, 4096], P(None, 'zero', 'width')
- new_momentum: float32 [128, 128, 4096], P(None, 'zero', 'width')
All inputs are finite; a program needn't handle non-finite values.
Results may differ from a plain program's by a relative error of at most 0.0001.
Values sent between devices are 32-bit elements; how exact they have to be, the bound alone decides.
A program may use at most 128 MiB of HBM per device.

v0:
```python
import jax
import jax.numpy as jnp
from jax import lax
from jax.sharding import PartitionSpec as P

ITERS = 3


hold_rate = 0.8
learn_rate = 0.8
decay_rate = 0.1


def body(slopes_in, moments_in, weights_in):
    new_momentum = hold_rate * moments_in + slopes_in
    direction = hold_rate * new_momentum + slopes_in
    moved = lax.all_to_all(direction, "zero", split_axis=0, concat_axis=1, tiled=True)
    total = lax.psum(jnp.sum(moved * moved, axis=(1, 2), keepdims=True), "width")
    iterate = moved * lax.rsqrt(total + 1e-06)
    for step in range(ITERS):
        gram = lax.psum(
            jnp.einsum("mik,mjk->mij", iterate, iterate, precision=lax.Precision.HIGHEST), "width"
        )
        mixed = -4.775 * gram + 2.0315 * jnp.einsum(
            "mij,mjk->mik", gram, gram, precision=lax.Precision.HIGHEST
        )
        iterate = 3.4445 * iterate + jnp.einsum(
            "mij,mjk->mik", mixed, iterate, precision=lax.Precision.HIGHEST
        )
    back = lax.all_to_all(iterate, "zero", split_axis=1, concat_axis=0, tiled=True)
    new_weights = (1.0 - learn_rate * decay_rate) * weights_in - learn_rate * back
    return (new_weights, new_momentum)


def solution(mesh):
    in_specs = (P(None, "zero", "width"), P(None, "zero", "width"), P(None, "zero", "width"))
    out_specs = (P(None, "zero", "width"), P(None, "zero", "width"))
    return jax.shard_map(body, mesh=mesh, in_specs=in_specs, out_specs=out_specs, check_vma=False)
```

profile of v0, /device:TPU:29, one launch (start us, length us, event | category | flops | bytes accessed | tf_op | source)
XLA Modules:
  0.0 608.0 jit_solution(12829300528116619400)
XLA Ops:
  7.2 0.0 all-reduce.4.cloned.1.call-start
  7.2 9.3 %multiply_add_fusion.3 = (f32[128,8,2048]{2,1,0:T(8,128)S(1)}, f32[128,8,2048]{2,1,0:T(8,128)}) fusion(f32[128,8,2048]{2,1,0:T(8,128)} %param.3, f32[128,8,2048]{2,1,0:T(8,128)} %param.4), kind=kLoop, calls=%fused_computation.7 | loop fusion | flops 8388608 | bytes 33554432 | tf_op jit(solution)/shard_map/add | solution.py:16
  16.5 188.0 %all_to_all.27 = f32[128,8,2048]{2,1,0:T(8,128)S(1)} all-to-all(f32[128,8,2048]{2,1,0:T(8,128)S(1)} %get-tuple-element.2), channel_id=1, replica_groups=mesh['zero'=16,'width'=2] {'zero'}, dimensions={0} | all-to-all | bytes 16777216 | tf_op jit(solution)/shard_map/all_to_all | solution.py:17
  204.5 0.0 copy-start
  204.5 3.4 copy-done
  207.9 0.8 fusion
  208.7 3.8 psum.28
  212.5 12.9 %fusion.2 = f32[8,128,128]{2,1,0:T(8,128)} fusion(f32[16,8,8,2048]{3,2,1,0:T(8,128)} %bitcast.38, f32[8]{0:T(128)S(1)} %rsqrt_bitcast_fusion), kind=kOutput, calls=%fused_computation.10 | convolution fusion | flops 3223322624 | bytes 8912928 | tf_op jit(solution)/shard_map/mik,mjk->mij/dot_general | solution.py:22
  225.4 0.0 all-reduce.4.cloned.1.call-update
  225.4 0.0 all-reduce.6.cloned.1.call-start
  225.5 30.1 %all-reduce.4.cloned.1.call-done = f32[8,128,128]{2,1,0:T(8,128)} async-done(((f32[8,128,128]{2,1,0:T(8,128)}), f32[8,128,128]{2,1,0:T(8,128)}) %all-reduce.4.cloned.1.call-update) | async-done | bytes 524304 | tf_op jit(solution)/shard_map/psum | solution.py:21
  255.6 2.1 fusion.7
  257.6 12.0 %multiply_add_fusion.2 = f32[8,128,2048]{2,1,0:T(8,128)S(1)} fusion(f32[16,8,8,2048]{3,2,1,0:T(8,128)} %bitcast.39, f32[8,128,128]{2,1,0:T(8,128)S(1)} %fusion.7, f32[8]{0:T(128)S(1)} %rsqrt_bitcast_fusion), kind=kOutput, calls=%fused_computation.6 | convolution fusion | flops 3229614080 | bytes 17301536 | tf_op jit(solution)/shard_map/mij,mjk->mik/dot_general | solution.py:27
  269.6 0.0 copy-start.1
  269.6 3.4 copy-done.1
  273.0 8.5 %fusion.8 = f32[8,128,128]{2,1,0:T(8,128)} fusion(f32[8,128,2048]{2,1,0:T(8,128)S(1)} %multiply_add_fusion.2), kind=kOutput, calls=%fused_computation.21 | convolution fusion | flops 3221225472 | bytes 8912896 | tf_op jit(solution)/shard_map/mik,mjk->mij/dot_general | solution.py:22
  281.5 0.0 all-reduce.6.cloned.1.call-update
  281.6 0.0 all-reduce.8.cloned.1.call-start
  281.6 28.8 %all-reduce.6.cloned.1.call-done = f32[8,128,128]{2,1,0:T(8,128)} async-done(((f32[8,128,128]{2,1,0:T(8,128)}), f32[8,128,128]{2,1,0:T(8,128)}) %all-reduce.6.cloned.1.call-update) | async-done | bytes 524304 | tf_op jit(solution)/shard_map/psum | solution.py:21
  310.4 2.1 fusion.6
  312.4 14.1 %multiply_add_fusion.1 = f32[8,128,2048]{2,1,0:T(8,128)S(1)} fusion(f32[8,128,2048]{2,1,0:T(8,128)} %copy-done.1, f32[8,128,128]{2,1,0:T(8,128)S(1)} %fusion.6), kind=kOutput, calls=%fused_computation.5 | convolution fusion | flops 3225419776 | bytes 17301504 | tf_op jit(solution)/shard_map/mij,mjk->mik/dot_general | solution.py:27
  326.5 0.0 copy-start.2
  326.5 3.4 copy-done.2
  329.9 8.5 %fusion.9 = f32[8,128,128]{2,1,0:T(8,128)} fusion(f32[8,128,2048]{2,1,0:T(8,128)S(1)} %multiply_add_fusion.1), kind=kOutput, calls=%fused_computation.22 | convolution fusion | flops 3221225472 | bytes 8912896 | tf_op jit(solution)/shard_map/mik,mjk->mij/dot_general | solution.py:22
  338.4 0.0 all-reduce.8.cloned.1.call-update
  338.5 28.8 %all-reduce.8.cloned.1.call-done = f32[8,128,128]{2,1,0:T(8,128)} async-done(((f32[8,128,128]{2,1,0:T(8,128)}), f32[8,128,128]{2,1,0:T(8,128)}) %all-reduce.8.cloned.1.call-update) | async-done | bytes 524304 | tf_op jit(solution)/shard_map/psum | solution.py:21
  367.3 2.1 fusion.5
  369.4 14.8 %multiply_add_fusion = f32[8,128,2048]{2,1,0:T(8,128)S(1)} fusion(f32[8,128,2048]{2,1,0:T(8,128)} %copy-done.2, f32[8,128,128]{2,1,0:T(8,128)S(1)} %fusion.5), kind=kOutput, calls=%fused_computation.4 | convolution fusion | flops 3225419776 | bytes 17301504 | tf_op jit(solution)/shard_map/mij,mjk->mik/dot_general | solution.py:27
  384.2 4.9 copy.8
  389.1 188.5 %all_to_all.28 = f32[8,128,2048]{2,0,1:T(8,128)S(1)} all-to-all(f32[8,128,2048]{2,0,1:T(8,128)S(1)} %copy.8), channel_id=1, replica_groups=mesh['zero'=16,'width'=2] {'zero'}, dimensions={1} | all-to-all | bytes 16777216 | tf_op jit(solution)/shard_map/all_to_all | solution.py:30
  577.5 1.8 broadcast_multiply_fusion
  579.3 9.7 %copy.9 = f32[16,8,8,2048]{3,2,1,0:T(8,128)} copy(f32[16,8,8,2048]{3,1,2,0:T(8,128)S(1)} %bitcast.40) | data formatting | bytes 16777216 | tf_op jit(solution)/shard_map/mul | solution.py:31
  589.1 12.0 %bitcast_subtract_fusion = f32[128,8,2048]{2,1,0:T(8,128)} fusion(f32[16,8,8,2048]{3,2,1,0:T(8,128)} %copy.9, f32[128,8,2048]{2,1,0:T(8,128)} %param.5), kind=kLoop, calls=%fused_computation.1 | loop fusion | flops 4194304 | bytes 25165824 | tf_op jit(solution)/shard_map/sub | solution.py:31
  (1 shorter events, 0.0 us)
Async XLA Ops:
  7.2 248.4 %all-reduce.4.cloned.1.call-start = ((), (), s32[]{:S(2)}) async-start(), calls=%async_computation.2 | async-start | bytes 1048576 | tf_op jit(solution)/shard_map/psum | solution.py:21
  204.5 3.4 copy-start
  225.4 85.0 %all-reduce.6.cloned.1.call-start = ((), (), s32[]{:S(2)}) async-start(), calls=%async_computation.3 | async-start | bytes 1048576 | tf_op jit(solution)/shard_map/psum | solution.py:21
  269.6 3.4 copy-start.1
  281.6 85.7 %all-reduce.8.cloned.1.call-start = ((), (), s32[]{:S(2)}) async-start(), calls=%async_computation.4 | async-start | bytes 1048576 | tf_op jit(solution)/shard_map/psum | solution.py:21
  326.5 3.4 copy-start.2
Sparse Core Ops, SparseCore 0:
  225.5 29.9 all-reduce.3
  281.7 28.6 all-reduce.5
  338.6 28.6 all-reduce.7
where the time goes:
time: 618 us; the launch traced here: 608 us
  blocking collectives  380 us (61%)
  waiting for transfers between devices  87.7 us (14%)
  matrix products  77 us (12%)
  local copies, waits for them, and re-layouts  24.7 us (4%)
  other arithmetic  23.9 us (4%)
  between operations  14.3 us (2%)
    all_to_all x1, blocking collectives, body(): lax.all_to_all(iterate, 'zero', split_axis=1, concat_axis=0, tiled=True)  188 us
    all_to_all x1, blocking collectives, body(): lax.all_to_all(direction, 'zero', split_axis=0, concat_axis=1, tiled=True)  188 us
    psum x3, waiting for transfers between devices, body(): lax.psum(jnp.einsum('mik,mjk->mij', iterate, iterate, precision=lax.Preci...  87.7 us
    dot_general x3, matrix products, body(): jnp.einsum('mij,mjk->mik', mixed, iterate, precision=lax.Precision.HIGHEST)  40.9 us
    dot_general x3, matrix products, body(): jnp.einsum('mik,mjk->mij', iterate, iterate, precision=lax.Precision.HIGH...  29.9 us
  transfers between devices with their start and end apart: 3, of which 3 were waited for; matrix products, arithmetic and copies ran while one was open for 0% of the time, Pallas kernels for 0%

commit v1 on v0

v1 whole, which is shorter than its diff:
```python
import functools

import jax
import jax.numpy as jnp
from jax import lax
from jax.experimental import pallas as pl
from jax.experimental.pallas import tpu as pltpu
from jax.sharding import PartitionSpec as P

ITERS = 3
MESH = pl.DeviceIdType.MESH

hold_rate = 0.8
learn_rate = 0.8
decay_rate = 0.1


def dot(a, b):
    return jnp.dot(a, b, precision=lax.Precision.HIGHEST, preferred_element_type=jnp.float32)


def kernel(nz, nw, sent, back, held, made, gram, heard, fwd_send, fwd_recv, gram_send, gram_recv, ret_send, ret_recv, own_sem):
    me = lax.axis_index("zero")
    side = lax.axis_index("width")
    mats, rows, cols = sent.shape
    mine = mats // nz
    total_rows = nz * rows

    barrier = pltpu.get_barrier_semaphore()

    def greet_zero(k, c):
        pl.semaphore_signal(barrier, inc=1, device_id=(lax.rem(me + k, nz), side), device_id_type=MESH)
        return c

    def greet_width(k, c):
        pl.semaphore_signal(barrier, inc=1, device_id=(me, lax.rem(side + k, nw)), device_id_type=MESH)
        return c

    lax.fori_loop(1, nz, greet_zero, 0)
    lax.fori_loop(1, nw, greet_width, 0)
    pl.semaphore_wait(barrier, nz - 1 + nw - 1)

    def forward(j, c):
        pltpu.make_async_copy(sent.at[me * mine + j], held.at[j, me], fwd_recv.at[j]).start()

        def one(k, c):
            to = lax.rem(me + k, nz)
            pltpu.make_async_remote_copy(
                src_ref=sent.at[to * mine + j],
                dst_ref=held.at[j, me],
                send_sem=fwd_send,
                recv_sem=fwd_recv.at[j],
                device_id=(to, side),
                device_id_type=MESH,
            ).start()
            return c

        return lax.fori_loop(1, nz, one, c)

    lax.fori_loop(0, mine, forward, 0)

    def gram_of(j):
        pltpu.make_async_copy(held.at[j], held.at[j], fwd_recv.at[j]).wait()
        x = held[j].reshape(total_rows, cols)
        gram[j] = lax.dot_general(
            x, x, (((1,), (1,)), ((), ())),
            precision=lax.Precision.HIGHEST, preferred_element_type=jnp.float32,
        )

        def one(k, c):
            to = lax.rem(side + k, nw)
            pltpu.make_async_remote_copy(
                src_ref=gram.at[j],
                dst_ref=heard.at[j, k - 1],
                send_sem=gram_send,
                recv_sem=gram_recv.at[j],
                device_id=(me, to),
                device_id_type=MESH,
            ).start()
            return c

        lax.fori_loop(1, nw, one, 0)

    def finish(j):
        pltpu.make_async_copy(heard.at[j], heard.at[j], gram_recv.at[j]).wait()
        full = gram[j] + jnp.sum(heard[j], axis=0)
        at_diag = lax.broadcasted_iota(jnp.int32, full.shape, 0) == lax.broadcasted_iota(jnp.int32, full.shape, 1)
        squares = jnp.sum(jnp.sum(jnp.where(at_diag, full, 0.0), axis=1, keepdims=True), axis=0, keepdims=True)
        scale = lax.rsqrt(squares + 1e-06)
        a = full * scale * scale
        eye = jnp.where(at_diag, 3.4445, 0.0)
        mix = None
        for step in range(ITERS):
            m = eye - 4.775 * a + 2.0315 * dot(a, a)
            if step < ITERS - 1:
                a = dot(dot(m, a), m)
            mix = m if mix is None else dot(m, mix)
        mix = mix * scale
        y = dot(mix, held[j].reshape(total_rows, cols))
        made[j] = y.reshape(nz, rows, cols)
        pltpu.make_async_copy(made.at[j, me], back.at[me * mine + j], own_sem).start()

        def one(k, c):
            to = lax.rem(me + k, nz)
            pltpu.make_async_remote_copy(
                src_ref=made.at[j, to],
                dst_ref=back.at[me * mine + j],
                send_sem=ret_send,
                recv_sem=ret_recv,
                device_id=(to, side),
                device_id_type=MESH,
            ).start()
            return c

        lax.fori_loop(1, nz, one, 0)

    gram_of(0)

    def stage(j, c):
        gram_of(j)
        finish(j - 1)
        return c

    lax.fori_loop(1, mine, stage, 0)
    finish(mine - 1)

    others = pl.ds(0, (nz - 1) * mine)
    own = pl.ds(0, mine)
    pltpu.make_async_copy(sent.at[others], sent.at[others], fwd_send).wait()
    pltpu.make_async_copy(heard, heard, gram_send).wait()
    pltpu.make_async_copy(back.at[others], back.at[others], ret_send).wait()
    pltpu.make_async_copy(back.at[others], back.at[others], ret_recv).wait()
    pltpu.make_async_copy(back.at[own], back.at[own], own_sem).wait()


def orthogonal(nz, nw, direction):
    mats, rows, cols = direction.shape
    mine = mats // nz
    n = nz * rows
    return pl.pallas_call(
        functools.partial(kernel, nz, nw),
        out_shape=jax.ShapeDtypeStruct(direction.shape, jnp.float32),
        in_specs=[pl.BlockSpec(memory_space=pltpu.HBM)],
        out_specs=pl.BlockSpec(memory_space=pltpu.HBM),
        scratch_shapes=[
            pltpu.VMEM((mine, nz, rows, cols), jnp.float32),
            pltpu.VMEM((mine, nz, rows, cols), jnp.float32),
            pltpu.VMEM((mine, n, n), jnp.float32),
            pltpu.VMEM((mine, nw - 1, n, n), jnp.float32),
            pltpu.SemaphoreType.DMA,
            pltpu.SemaphoreType.DMA((mine,)),
            pltpu.SemaphoreType.DMA,
            pltpu.SemaphoreType.DMA((mine,)),
            pltpu.SemaphoreType.DMA,
            pltpu.SemaphoreType.DMA,
            pltpu.SemaphoreType.DMA,
        ],
        compiler_params=pltpu.CompilerParams(
            collective_id=0, has_side_effects=True, vmem_limit_bytes=48 * 1024 * 1024
        ),
        name="orthogonal",
    )(direction)


def body(nz, nw, slopes_in, moments_in, weights_in):
    new_momentum = hold_rate * moments_in + slopes_in
    direction = hold_rate * new_momentum + slopes_in
    back = orthogonal(nz, nw, direction)
    new_weights = (1.0 - learn_rate * decay_rate) * weights_in - learn_rate * back
    return (new_weights, new_momentum)


def solution(mesh):
    spec = P(None, "zero", "width")
    run = functools.partial(body, mesh.shape["zero"], mesh.shape["width"])
    return jax.shard_map(run, mesh=mesh, in_specs=(spec,) * 3, out_specs=(spec,) * 2, check_vma=False)
```

time: 618 us -> 392 us (0.63); the launches traced: 608 us -> 391 us
  blocking collectives: 380 us -> 0 us
  Pallas kernels: 0 us -> 367 us
  waiting for transfers between devices: 87.7 us -> 0 us
  matrix products: 77 us -> 0 us
  local copies, waits for them, and re-layouts: 24.7 us -> 0 us
  between operations: 14.3 us -> 0.64 us
    all_to_all x2 -> x0, blocking collectives: 377 us -> none  [the longest x1 188 us: body(): lax.all_to_all(iterate, 'zero', split_axis=1, concat_axis=0, tiled=True)]
    pallas_call x0 -> x1, Pallas kernels: none -> 367 us  [orthogonal(): pl.pallas_call(functools.partial(kernel, nz, nw), out_shape=jax.ShapeDtyp...]
    psum x3 -> x0, waiting for transfers between devices: 87.7 us -> none  [body(): lax.psum(jnp.einsum('mik,mjk->mij', iterate, iterate, precision=lax.Preci...]
    dot_general x9 -> x0, matrix products: 77 us -> none  [the longest x3 40.9 us: body(): jnp.einsum('mij,mjk->mik', mixed, iterate, precision=lax.Precision.HIGHEST)]
    unnamed x6 -> x0, local copies, waits for them, and re-layouts: 10.2 us -> none
    mul x1 -> x0, local copies, waits for them, and re-layouts: 9.71 us -> none  [body(): learn_rate * back]
  transfers between devices with their start and end apart: 3 -> 0, of which waited for: 3 -> 0; matrix products, arithmetic and copies ran while one was open for 0% -> 0% of each run, Pallas kernels for 0% -> 0%
where the time goes in v1:
time: 392 us; the launch traced here: 391 us
  Pallas kernels  367 us (94%)
  other arithmetic  23.4 us (6%)
    pallas_call x1, Pallas kernels, orthogonal(): pl.pallas_call(functools.partial(kernel, nz, nw), out_shape=jax.ShapeDtyp...  367 us
    sub x1, other arithmetic, body(): (1.0 - learn_rate * decay_rate) * weights_in - learn_rate * back  12.1 us
    add x1, other arithmetic, body(): direction = hold_rate * new_momentum + slopes_in  11.3 us

profile of v1, /device:TPU:29, one launch (start us, length us, event | category | flops | bytes accessed | tf_op | source)
XLA Modules:
  0.0 391.4 jit_solution(5730687405955467512)
XLA Ops:
  0.6 11.3 %multiply_add_fusion = (f32[128,8,2048]{2,1,0:T(8,128)}, f32[128,8,2048]{2,1,0:T(8,128)}) fusion(f32[128,8,2048]{2,1,0:T(8,128)} %param.3, f32[128,8,2048]{2,1,0:T(8,128)} %param.4), kind=kLoop, calls=%fused_computation.1 | loop fusion | flops 8388608 | bytes 33554432 | tf_op jit(solution)/shard_map/add | solution.py:167
  11.9 367.3 %orthogonal.1 = f32[128,8,2048]{2,1,0:T(8,128)} custom-call(f32[128,8,2048]{2,1,0:T(8,128)} %get-tuple-element.2.sent), custom_call_target="tpu_custom_call" | custom-call | tf_op jit(solution)/shard_map/orthogonal/pallas_call | solution.py:140
  379.3 12.1 %multiply_subtract_fusion = f32[128,8,2048]{2,1,0:T(8,128)} fusion(f32[128,8,2048]{2,1,0:T(8,128)} %orthogonal.1, f32[128,8,2048]{2,1,0:T(8,128)} %param.5), kind=kLoop, calls=%fused_computation | loop fusion | flops 6291456 | bytes 25165824 | tf_op jit(solution)/shard_map/sub | solution.py:169

commit v2 on v1

--- a/solution.py
+++ b/solution.py
@@ -19,7 +19,10 @@
     return jnp.dot(a, b, precision=lax.Precision.HIGHEST, preferred_element_type=jnp.float32)
 
 
-def kernel(nz, nw, sent, back, held, made, gram, heard, fwd_send, fwd_recv, gram_send, gram_recv, ret_send, ret_recv, own_sem):
+def kernel(
+    nz, nw, sent, weights, new_weights, held, made, back, old, gram, heard,
+    fwd_send, fwd_recv, gram_send, gram_recv, ret_send, ret_recv, old_sem, new_sem,
+):
     me = lax.axis_index("zero")
     side = lax.axis_index("width")
     mats, rows, cols = sent.shape
@@ -58,6 +61,7 @@
         return lax.fori_loop(1, nz, one, c)
 
     lax.fori_loop(0, mine, forward, 0)
+    pltpu.make_async_copy(weights, old, old_sem).start()
 
     def gram_of(j):
         pltpu.make_async_copy(held.at[j], held.at[j], fwd_recv.at[j]).wait()
@@ -98,7 +102,6 @@
         mix = mix * scale
         y = dot(mix, held[j].reshape(total_rows, cols))
         made[j] = y.reshape(nz, rows, cols)
-        pltpu.make_async_copy(made.at[j, me], back.at[me * mine + j], own_sem).start()
 
         def one(k, c):
             to = lax.rem(me + k, nz)
@@ -106,13 +109,14 @@
                 src_ref=made.at[j, to],
                 dst_ref=back.at[me * mine + j],
                 send_sem=ret_send,
-                recv_sem=ret_recv,
+                recv_sem=ret_recv.at[j],
                 device_id=(to, side),
                 device_id_type=MESH,
             ).start()
             return c
 
         lax.fori_loop(1, nz, one, 0)
+        back[me * mine + j] = made[j, me]
 
     gram_of(0)
 
@@ -124,27 +128,48 @@
     lax.fori_loop(1, mine, stage, 0)
     finish(mine - 1)
 
+    pltpu.make_async_copy(weights, old, old_sem).wait()
+
+    def update(j, c):
+        came = back.at[pl.ds(0, nz - 1)]
+        pltpu.make_async_copy(came, came, ret_recv.at[j]).wait()
+
+        def one(k, c):
+            at = k * mine + j
+            back[at] = (1.0 - learn_rate * decay_rate) * old[at] - learn_rate * back[at]
+            return c
+
+        def leave(k, c):
+            at = k * mine + j
+            pltpu.make_async_copy(back.at[at], new_weights.at[at], new_sem).start()
+            return c
+
+        lax.fori_loop(0, nz, one, 0)
+        return lax.fori_loop(0, nz, leave, c)
+
+    lax.fori_loop(0, mine, update, 0)
+
     others = pl.ds(0, (nz - 1) * mine)
-    own = pl.ds(0, mine)
     pltpu.make_async_copy(sent.at[others], sent.at[others], fwd_send).wait()
     pltpu.make_async_copy(heard, heard, gram_send).wait()
     pltpu.make_async_copy(back.at[others], back.at[others], ret_send).wait()
-    pltpu.make_async_copy(back.at[others], back.at[others], ret_recv).wait()
-    pltpu.make_async_copy(back.at[own], back.at[own], own_sem).wait()
-
-
-def orthogonal(nz, nw, direction):
+    pltpu.make_async_copy(back, new_weights, new_sem).wait()
+
+
+def stepped(nz, nw, direction, weights):
     mats, rows, cols = direction.shape
     mine = mats // nz
     n = nz * rows
     return pl.pallas_call(
         functools.partial(kernel, nz, nw),
         out_shape=jax.ShapeDtypeStruct(direction.shape, jnp.float32),
-        in_specs=[pl.BlockSpec(memory_space=pltpu.HBM)],
+        in_specs=[pl.BlockSpec(memory_space=pl.ANY), pl.BlockSpec(memory_space=pltpu.HBM)],
         out_specs=pl.BlockSpec(memory_space=pltpu.HBM),
         scratch_shapes=[
             pltpu.VMEM((mine, nz, rows, cols), jnp.float32),
             pltpu.VMEM((mine, nz, rows, cols), jnp.float32),
+            pltpu.VMEM(direction.shape, jnp.float32),
+            pltpu.VMEM(direction.shape, jnp.float32),
             pltpu.VMEM((mine, n, n), jnp.float32),
             pltpu.VMEM((mine, nw - 1, n, n), jnp.float32),
             pltpu.SemaphoreType.DMA,
@@ -152,21 +177,21 @@
             pltpu.SemaphoreType.DMA,
             pltpu.SemaphoreType.DMA((mine,)),
             pltpu.SemaphoreType.DMA,
+            pltpu.SemaphoreType.DMA((mine,)),
             pltpu.SemaphoreType.DMA,
             pltpu.SemaphoreType.DMA,
         ],
         compiler_params=pltpu.CompilerParams(
-            collective_id=0, has_side_effects=True, vmem_limit_bytes=48 * 1024 * 1024
+            collective_id=0, has_side_effects=True, vmem_limit_bytes=38 * 1024 * 1024
         ),
-        name="orthogonal",
-    )(direction)
+        name="stepped",
+    )(direction, weights)
 
 
 def body(nz, nw, slopes_in, moments_in, weights_in):
     new_momentum = hold_rate * moments_in + slopes_in
     direction = hold_rate * new_momentum + slopes_in
-    back = orthogonal(nz, nw, direction)
-    new_weights = (1.0 - learn_rate * decay_rate) * weights_in - learn_rate * back
+    new_weights = stepped(nz, nw, direction, weights_in)
     return (new_weights, new_momentum)
 
 

time: 392 us -> 384 us (0.980)
  other arithmetic: 23.4 us -> 11.3 us
    sub x1 -> x0, other arithmetic: 12.1 us -> none  [body(): (1.0 - learn_rate * decay_rate) * weights_in - learn_rate * back]
where the time goes in v2:
time: 384 us
  Pallas kernels  369 us (96%)
  other arithmetic  11.3 us (3%)
    pallas_call x1, Pallas kernels, stepped(): pl.pallas_call(functools.partial(kernel, nz, nw), out_shape=jax.ShapeDtyp...  369 us
    add x1, other arithmetic, body(): direction = hold_rate * new_momentum + slopes_in  11.3 us

profile of v2, /device:TPU:29, one launch (start us, length us, event | category | flops | bytes accessed | tf_op | source)
XLA Modules:
  0.0 384.3 jit_solution(9001984215896335340)
XLA Ops:
  0.6 11.3 %multiply_add_fusion = (f32[128,8,2048]{2,1,0:T(8,128)}, f32[128,8,2048]{2,1,0:T(8,128)}) fusion(f32[128,8,2048]{2,1,0:T(8,128)} %param.3, f32[128,8,2048]{2,1,0:T(8,128)} %param.4), kind=kLoop, calls=%fused_computation | loop fusion | flops 8388608 | bytes 33554432 | tf_op jit(solution)/shard_map/add | solution.py:193
  11.9 369.0 %stepped.1 = f32[128,8,2048]{2,1,0:T(8,128)S(1)} custom-call(f32[128,8,2048]{2,1,0:T(8,128)} %get-tuple-element.2.sent, f32[128,8,2048]{2,1,0:T(8,128)} %weights.1), custom_call_target="tpu_custom_call" | custom-call | tf_op jit(solution)/shard_map/stepped/pallas_call | solution.py:163
  380.9 3.4 copy.6
